TPU v7x, 32 devices: a whole 2x2x4 slice. The times are simulated.
32 devices in a mesh: slab: 16 (over z, x, core), tile: 2 (over y).
Axes of the slice: x: 2, y: 2, z: 4, core: 2. Of those that a mesh axis runs over, the one named last changes fastest.
Arguments:
- features: bfloat16 [16, 2, 512, 128], P('slab', 'tile'), may hold values from -24 to 24
- counts: int32 [16, 2], P('slab', 'tile'), may hold values from 128 to 512, as said below
- rulebook: int32 [16, 2, 27, 512], P('slab', 'tile'), may hold values from 0 to 800, as said below
- face_rows: int32 [16, 2, 4, 64], P('slab', 'tile'), may hold values from 0 to 511, as said below
- conv_one: bfloat16 [27, 128, 128], replicated, may hold values from -0.109375 to 0.109375
- gain_one: float32 [128], replicated, may hold values from 0.5 to 1.5
- shift_one: float32 [128], replicated, may hold values from -0.5 to 0.5
- conv_two: bfloat16 [27, 128, 128], replicated, may hold values from -0.109375 to 0.109375
- gain_two: float32 [128], replicated, may hold values from 0.5 to 1.5
- shift_two: float32 [128], replicated, may hold values from -0.5 to 0.5
Outputs:
- output: bfloat16 [16, 2, 512, 128], P('slab', 'tile')
Inputs may be any that keep to these rules, and one draw needn't show every extreme that they name: `counts`: each device's voxels fill its 8 x 8 grid columns with the same number each, between 2 and 8; some device of the highest slab index holds 512. `rulebook`: an entry names the extended-table row that holds the voxel's neighbour at offset k = 9 (dx + 1) + 3 (dy + 1) + (dz + 1) of the submanifold 3x3x3 stencil, or 800 where that cell is inactive or outside the grid; the voxel itself is at offset 13; rows at or past the device's count name 800 at every offset. `face_rows`: lists 0 to 3 hold the device's voxels on its lower and higher face along the first, then the lower and higher face along the second dimension; the j-th voxel of the i-th column along a face stands at position i * 8 + j; unused positions name row 0.
All inputs are finite; a program needn't handle non-finite values.
Results may differ from a plain program's by a relative error of at most 0.0033.
Values may be sent and summed in bfloat16 or wider, within the bound.
A program may use at most 64 MiB of HBM per device.

v0:
```python
from functools import partial

import jax
import jax.numpy as jnp
from jax import lax
from jax.experimental import pallas as pl
from jax.experimental.pallas import tpu as pltpu
from jax.sharding import PartitionSpec as P

SIDE = 8
EPSILON = 1e-05
MESH = pl.DeviceIdType.MESH
BLOCK = 256
PIECE = 16
F32 = jnp.float32
BF16 = jnp.bfloat16


def transfers(face_len):
    low, high = 0, face_len
    edge = face_len - PIECE
    end = PIECE + face_len
    return (
        (1, 0, high, face_len, 0, 0),
        (-1, 0, low, face_len, 0, face_len),
        (0, 1, 3 * face_len, face_len, 1, PIECE),
        (0, -1, 2 * face_len, face_len, 2, PIECE),
        (1, 1, high + edge, PIECE, 1, 0),
        (-1, 1, low + edge, PIECE, 1, end),
        (1, -1, high, PIECE, 2, 0),
        (-1, -1, low, PIECE, 2, end),
    )


def block_kernel(
    n_slab,
    n_tile,
    feat_hbm,
    count_ref,
    rule_hbm,
    face_hbm,
    gain_one_hbm,
    shift_one_hbm,
    gain_two_hbm,
    shift_two_hbm,
    conv_one_ref,
    conv_two_ref,
    out_ref,
    feat_ref,
    rule_ref,
    face_ref,
    gain_one_ref,
    shift_one_ref,
    gain_two_ref,
    shift_two_ref,
    weight_ref,
    weight_t_ref,
    onehot_ref,
    part_ref,
    keep_ref,
    face_hot_ref,
    square_ref,
    slope_ref,
    own_ref,
    send_ref,
    wide_send_ref,
    halo_ref,
    wide_halo_ref,
    lhs_ref,
    picked_ref,
    stats_ref,
    counts_ref,
    input_sem,
    send_sem,
    recv_sem,
    stat_send_sem,
    stat_recv_sem,
):
    rows, channels = feat_ref.shape
    taps = rule_ref.shape[0]
    face_len = face_ref.shape[1]
    column = face_len // SIDE
    n_dev = n_slab * n_tile
    blocks = rows // BLOCK
    group = taps // 3
    slab = lax.axis_index("slab")
    tile = lax.axis_index("tile")
    me = slab * n_tile + tile

    def fetch(i, src, dst):
        return pltpu.make_async_copy(src, dst, input_sem.at[i])

    input_copies = [
        fetch(0, feat_hbm, feat_ref),
        fetch(1, face_hbm, face_ref),
        fetch(2, rule_hbm, rule_ref),
    ]
    affine_copies = [
        fetch(3, gain_one_hbm, gain_one_ref),
        fetch(4, shift_one_hbm, shift_one_ref),
        fetch(5, gain_two_hbm, gain_two_ref),
        fetch(6, shift_two_hbm, shift_two_ref),
    ]
    weight_copies = [
        fetch(7, conv_one_ref, weight_ref.at[0]),
        fetch(8, conv_two_ref, weight_ref.at[1]),
    ]
    for copy in (input_copies[1], input_copies[0], input_copies[2]):
        copy.start()
    halo_ref[...] = jnp.zeros_like(halo_ref)
    wide_halo_ref[...] = jnp.zeros_like(wide_halo_ref)

    def moved(place, step, size):
        if size & (size - 1) == 0:
            return place ^ step
        place = place + step
        return jnp.where(place >= size, place - size, place)

    def each_peer(act):
        for j in reversed(range(n_tile)):
            other = moved(tile, j, n_tile) if j else tile

            def visit(i, carry):
                act({"slab": moved(slab, n_slab - 1 - i, n_slab), "tile": other})
                return carry

            last = n_slab if j else n_slab - 1
            lax.fori_loop(0, last, visit, 0, unroll=n_slab <= 16)

    barrier = pltpu.get_barrier_semaphore()

    each_peer(
        lambda peer: pl.semaphore_signal(
            barrier, inc=1, device_id=peer, device_id_type=MESH
        )
    )
    for copy in weight_copies + affine_copies:
        copy.start()

    def halo(which, start):
        source, target = ((send_ref, halo_ref), (wide_send_ref, wide_halo_ref))[which]
        for j, (ds, dt, first, size, buffer, place) in enumerate(transfers(face_len)):
            copy = pltpu.make_async_remote_copy(
                src_ref=source.at[pl.ds(first, size)],
                dst_ref=target.at[buffer, pl.ds(place, size)],
                send_sem=send_sem.at[which, j],
                recv_sem=recv_sem.at[which, j],
                device_id={"slab": slab + ds, "tile": tile + dt},
                device_id_type=MESH,
            )
            sends, receives = True, True
            if ds > 0:
                sends, receives = slab < n_slab - 1, slab > 0
            elif ds < 0:
                sends, receives = slab > 0, slab < n_slab - 1
            if dt > 0:
                sends, receives = sends & (tile < n_tile - 1), receives & (tile > 0)
            elif dt < 0:
                sends, receives = sends & (tile > 0), receives & (tile < n_tile - 1)
            if start:
                pl.when(sends)(copy.start)
            else:
                pl.when(receives)(copy.wait_recv)
                pl.when(sends)(copy.wait_send)

    input_copies[1].wait()
    square_ref[...] = jnp.zeros_like(square_ref)
    square_ref[0:4, 0:face_len] = face_ref[...].astype(F32)
    face_cols = square_ref[...].T
    lane_rows = lax.broadcasted_iota(jnp.int32, (face_len, rows), 1)
    for k in range(4):
        wanted = face_cols[0:face_len, k : k + 1].astype(jnp.int32)
        face_hot_ref[k * face_len : (k + 1) * face_len, :] = jnp.where(
            lane_rows == wanted, 1.0, 0.0
        ).astype(BF16)

    input_copies[0].wait()
    feat = feat_ref[...]
    send_ref[...] = jnp.dot(face_hot_ref[...], feat, preferred_element_type=F32).astype(BF16)

    input_copies[2].wait()
    rule = rule_ref[...]
    tile_len = face_len + 2 * column
    below = rows + 2 * face_len
    above = below + tile_len
    q_low = rule - below
    q_high = rule - above
    base = 2 * face_len + PIECE - column
    skip = PIECE - column
    place_low = base + q_low + jnp.where(q_low >= column + face_len, skip, 0)
    place_high = base + q_high - jnp.where(q_high < column, skip, 0)
    place = jnp.where(
        rule < rows,
        rule & (BLOCK - 1),
        jnp.where(
            rule < below, rule - rows, jnp.where(rule < above, place_low, place_high)
        ),
    )
    part = jnp.where(
        rule < rows, rule // BLOCK, jnp.where(rule < above + tile_len, blocks, blocks + 1)
    )
    part_ref[...] = part
    dead = (part > blocks) | ((rule < rows) & (rule >= count_ref[0, 0]))
    keep_ref[...] = jnp.where(dead, 0, 1)
    position = lax.broadcasted_iota(jnp.int32, (BLOCK, rows), 0).astype(F32).astype(BF16)
    place = place.astype(F32).astype(BF16)
    one, none = jnp.ones((BLOCK, rows), BF16), jnp.zeros((BLOCK, rows), BF16)
    for k in range(taps):
        onehot_ref[k] = jnp.where(position == place[k], one, none)

    count = count_ref[0, 0]
    live = (lax.broadcasted_iota(jnp.int32, (rows, 1), 0) < count).astype(F32)

    def share(which, buffer):
        mine = buffer.at[me]
        each_peer(
            lambda peer: pltpu.make_async_remote_copy(
                src_ref=mine,
                dst_ref=mine,
                send_sem=stat_send_sem.at[which],
                recv_sem=stat_recv_sem.at[which],
                device_id=peer,
                device_id_type=MESH,
            ).start()
        )

    def shared(which, buffer):
        others = buffer.at[pl.ds(0, n_dev - 1)]
        pltpu.make_async_copy(others, others, stat_recv_sem.at[which]).wait()
        pltpu.make_async_copy(others, others, stat_send_sem.at[which]).wait()
        return jnp.sum(buffer[...], axis=0)

    counts_ref[me] = jnp.full((1, channels), count.astype(F32))
    pl.semaphore_wait(barrier, n_dev - 1)
    halo(0, True)
    share(2, counts_ref)

    def load_local(values):
        for b in range(blocks):
            turned = values[b * BLOCK : (b + 1) * BLOCK].T
            for y in range(3):
                lhs_ref[y, b * channels : (b + 1) * channels, :] = turned

    def load_halo(pieces):
        turned = [piece.T for piece in pieces]
        low = blocks * channels
        half = BLOCK // 2
        for y, other in ((0, turned[1]), (1, None), (2, turned[2])):
            lhs_ref[y, low:, 0:half] = turned[0]
            lhs_ref[y, low:, half:] = jnp.zeros_like(turned[0]) if other is None else other

    load_local(feat)
    def turn_weights(i):
        weight_copies[i].wait()
        for x in range(3):
            weight_t_ref[i, x] = weight_ref[i, x * group * channels : (x + 1) * group * channels, :].T

    turn_weights(0)

    def choose(home, found, value, chosen):
        for i, b in enumerate(chosen):
            value = jnp.where(home == b, found[i * channels : (i + 1) * channels], value)
        return value

    def pick_local(x, carry):
        for j in range(group):
            tap = x * group + j
            found = jnp.dot(
                lhs_ref[0, 0 : blocks * channels], onehot_ref[tap], preferred_element_type=F32
            )
            value = choose(part_ref[tap], found, jnp.zeros((channels, rows), F32), range(blocks))
            picked_ref[tap] = value.astype(BF16)
        return carry

    def pick_halo(tap, j):
        found = jnp.dot(
            lhs_ref[j // 3, blocks * channels :], onehot_ref[tap], preferred_element_type=F32
        )
        value = choose(part_ref[tap], found, picked_ref[tap].astype(F32), (blocks,))
        picked_ref[tap] = value.astype(BF16)

    def pick_halos(x):
        for j in range(group):
            if x != 1 or j // 3 != 1:
                pick_halo(x * group + j, j)

    def multiply(which, x, total):
        taken = picked_ref[pl.ds(x * group, group)].reshape(group * channels, rows)
        return total + jnp.dot(weight_t_ref[which, x], taken, preferred_element_type=F32)

    def tell_sums(which, values):
        kept = values * live
        stats_ref[which, me] = jnp.concatenate(
            [
                jnp.sum(kept, axis=0, keepdims=True),
                jnp.sum(kept * values, axis=0, keepdims=True),
            ],
            axis=0,
        )
        share(which, stats_ref.at[which])
        return stats_ref[which, me][0:1] / count.astype(F32)

    def affine(which, voxels, gain_ref, shift_ref):
        total = shared(which, stats_ref.at[which])
        average = total[0:1] / voxels
        variance = total[1:2] / voxels - average * average
        scale = lax.rsqrt(variance + EPSILON) * gain_ref[...]
        return scale, shift_ref[...] - average * scale

    lax.fori_loop(0, 3, pick_local, 0)
    halo(0, False)
    load_halo([halo_ref[i] for i in range(3)])
    blank = jnp.zeros((channels, rows), F32)
    first = blank
    for x in range(3):
        pick_halos(x)
        first = multiply(0, x, first)
    first = first.T
    centre = tell_sums(0, first)
    coarse = first.astype(BF16)
    fine = (first - coarse.astype(F32)).astype(BF16)
    both = jnp.dot(
        face_hot_ref[...],
        jnp.concatenate([coarse, fine], axis=1),
        preferred_element_type=F32,
    )
    wide_send_ref[...] = both[:, 0:channels] + both[:, channels:]
    halo(1, True)
    centred = first - centre
    for b in range(blocks):
        turned = centred[b * BLOCK : (b + 1) * BLOCK].T
        own_ref[:, b * BLOCK : (b + 1) * BLOCK] = turned
        lhs_ref[0, b * channels : (b + 1) * channels, :] = turned.astype(BF16)
    lax.fori_loop(0, 3, pick_local, 0)
    turn_weights(1)
    halo(1, False)
    load_halo([(wide_halo_ref[i] - centre).astype(BF16) for i in range(3)])
    for x in range(3):
        pick_halos(x)
    for copy in affine_copies:
        copy.wait()
    voxels = shared(2, counts_ref)
    scale, offset = affine(0, voxels, gain_one_ref, shift_one_ref)

    square_ref[...] = jnp.broadcast_to(scale, (channels, channels)).T
    slope_ref[...] = jnp.broadcast_to(centre * scale + offset, (channels, channels)).T

    def convolve_two(x, total):
        slope = jnp.concatenate([square_ref[...]] * (rows // channels), axis=1)
        level = jnp.concatenate([slope_ref[...]] * (rows // channels), axis=1)
        for j in range(group):
            tap = x * group + j
            value = picked_ref[tap].astype(F32)
            if j == group // 2:
                middle = jnp.full((channels, rows), x, jnp.int32) == 1
                value = jnp.where(middle, own_ref[...], value)
            value = jnp.maximum(value * slope + level, 0.0)
            value = jnp.where(keep_ref[tap] > 0, value, 0.0)
            picked_ref[tap] = value.astype(BF16)
        return multiply(1, x, total)

    second = lax.fori_loop(0, 3, convolve_two, blank).T
    tell_sums(1, second)
    scale, offset = affine(1, voxels, gain_two_ref, shift_two_ref)
    summed = second * scale + offset + feat_ref[...].astype(F32)
    out_ref[...] = (live * jnp.maximum(summed, 0.0)).astype(BF16)


def per_device(
    n_slab,
    n_tile,
    features,
    counts,
    rulebook,
    face_rows,
    conv_one,
    gain_one,
    shift_one,
    conv_two,
    gain_two,
    shift_two,
):
    rows, channels = features.shape[2:]
    taps = rulebook.shape[2]
    faces, face_len = face_rows.shape[2:]
    blocks = rows // BLOCK
    smem = pl.BlockSpec(memory_space=pltpu.SMEM)
    vmem = pl.BlockSpec(memory_space=pltpu.VMEM)
    hbm = pl.BlockSpec(memory_space=pltpu.HBM)
    group = taps // 3 * channels
    output = pl.pallas_call(
        partial(block_kernel, n_slab, n_tile),
        out_shape=jax.ShapeDtypeStruct((rows, channels), features.dtype),
        in_specs=[hbm, smem] + [hbm] * 8,
        out_specs=vmem,
        scratch_shapes=[
            pltpu.VMEM((rows, channels), BF16),
            pltpu.VMEM((taps, 1, rows), jnp.int32),
            pltpu.VMEM((faces, face_len), jnp.int32),
            pltpu.VMEM((1, channels), F32),
            pltpu.VMEM((1, channels), F32),
            pltpu.VMEM((1, channels), F32),
            pltpu.VMEM((1, channels), F32),
            pltpu.VMEM((2, taps * channels, channels), BF16),
            pltpu.VMEM((2, 3, channels, group), BF16),
            pltpu.VMEM((taps, BLOCK, rows), BF16),
            pltpu.VMEM((taps, 1, rows), jnp.int32),
            pltpu.VMEM((taps, 1, rows), jnp.int32),
            pltpu.VMEM((faces * face_len, rows), BF16),
            pltpu.VMEM((channels, channels), F32),
            pltpu.VMEM((channels, channels), F32),
            pltpu.VMEM((channels, rows), F32),
            pltpu.VMEM((faces * face_len, channels), BF16),
            pltpu.VMEM((faces * face_len, channels), F32),
            pltpu.VMEM((3, BLOCK // 2, channels), BF16),
            pltpu.VMEM((3, BLOCK // 2, channels), F32),
            pltpu.VMEM((3, (blocks + 1) * channels, BLOCK), BF16),
            pltpu.VMEM((taps, channels, rows), BF16),
            pltpu.VMEM((2, n_slab * n_tile, 2, channels), F32),
            pltpu.VMEM((n_slab * n_tile, 1, channels), F32),
            pltpu.SemaphoreType.DMA((9,)),
            pltpu.SemaphoreType.DMA((2, 8)),
            pltpu.SemaphoreType.DMA((2, 8)),
            pltpu.SemaphoreType.DMA((3,)),
            pltpu.SemaphoreType.DMA((3,)),
        ],
        compiler_params=pltpu.CompilerParams(
            collective_id=0, has_side_effects=True, vmem_limit_bytes=63200000
        ),
    )(
        features[0, 0],
        counts,
        rulebook.reshape(taps, 1, rows),
        face_rows[0, 0],
        gain_one[None],
        shift_one[None],
        gain_two[None],
        shift_two[None],
        conv_one.reshape(taps * channels, channels),
        conv_two.reshape(taps * channels, channels),
    )
    return output[None, None]


def solution(mesh):
    placed = (
        P("slab", "tile", None, None),
        P("slab", "tile"),
        P("slab", "tile", None, None),
        P("slab", "tile", None, None),
        P(),
        P(),
        P(),
        P(),
        P(),
        P(),
    )
    return jax.shard_map(
        partial(per_device, mesh.shape["slab"], mesh.shape["tile"]),
        mesh=mesh,
        in_specs=placed,
        out_specs=P("slab", "tile", None, None),
        check_vma=False,
    )
```

profile of v0, /device:TPU:0, one launch (start us, length us, event | category | flops | bytes accessed | tf_op | source)
XLA Modules:
  0.0 26.3 jit_solution(12150368653012623674)
XLA Ops:
  0.7 24.1 %shard_map.100 = bf16[512,128]{1,0:T(8,128)(2,1)} custom-call(bf16[512,128]{1,0:T(8,128)(2,1)} %bitcast.13, s32[1,1]{1,0:T(1,128)S(6)} %copy.12.count_ref, s32[27,1,512]{2,1,0:T(1,128)} %bitcast.14, s32[4,64]{1,0:T(4,128)} %bitcast.15, f32[1,128]{1,0:T(1,128)} %bitcast.16, f32[1,128]{1,0:T(1,128)} %bitcast.17, f32[1,128]{1,0:T(1,128)} %bitcast.18, ...), custom_call_target="tpu_custom_call" | custom-call | tf_op jit(solution)/shard_map/pallas_call | solution.py:391
  24.8 1.6 %copy.13 = bf16[1,1,512,128]{3,2,1,0:T(8,128)(2,1)} copy(bf16[1,1,512,128]{3,2,1,0:T(8,128)(2,1)} %bitcast.12) | data formatting | bytes 262144
where the time goes:
time: 26.5 us; the launch traced here: 26.3 us
  Pallas kernels  24.1 us (91%)
  local copies, waits for them, and re-layouts  1.57 us (6%)
  between operations  0.66 us (2%)
    pallas_call x1, Pallas kernels, per_device(): pl.pallas_call(partial(block_kernel, n_slab, n_tile), out_shape=jax.Shape...  24.1 us
    unnamed x1, local copies, waits for them, and re-layouts  1.57 us

commit v1 on v0

--- a/solution.py
+++ b/solution.py
@@ -425,7 +425,7 @@
             pltpu.SemaphoreType.DMA((3,)),
         ],
         compiler_params=pltpu.CompilerParams(
-            collective_id=0, has_side_effects=True, vmem_limit_bytes=63200000
+            collective_id=0, has_side_effects=True, vmem_limit_bytes=30000000
         ),
     )(
         features[0, 0],

time: 26.5 us -> 30 us (1.13)
  local copies, waits for them, and re-layouts: 1.57 us -> 5.39 us
  Pallas kernels: 24.1 us -> 23.6 us
    unnamed x1 -> x19, local copies, waits for them, and re-layouts: 1.57 us -> 5.39 us
    pallas_call x1, Pallas kernels: 24.1 us -> 23.6 us  [per_device(): pl.pallas_call(partial(block_kernel, n_slab, n_tile), out_shape=jax.Shape...]
where the time goes in v1:
time: 30 us; the launch traced here: 29.7 us
  Pallas kernels  23.6 us (79%)
  local copies, waits for them, and re-layouts  5.39 us (18%)
  between operations  0.71 us (2%)
    pallas_call x1, Pallas kernels, per_device(): pl.pallas_call(partial(block_kernel, n_slab, n_tile), out_shape=jax.Shape...  23.6 us
    unnamed x19, local copies, waits for them, and re-layouts  5.39 us

profile of v1, /device:TPU:0, one launch (start us, length us, event | category | flops | bytes accessed | tf_op | source)
XLA Modules:
  0.0 29.7 jit_solution(7908972787807248809)
XLA Ops:
  0.7 0.0 copy-start.8
  0.7 0.0 copy-start.4
  0.7 0.0 copy-start.5
  0.7 0.0 copy-start.6
  0.7 0.0 copy-start.7
  0.7 0.6 %copy-done.8 = f32[128]{0:T(128)S(1)} copy-done((f32[128]{0:T(128)S(1)}, f32[128]{0:T(128)}, u32[]{:S(2)}) %copy-start.8) | copy-done | bytes 536
  1.3 0.0 copy-done.4
  1.4 0.0 copy-done.5
  1.4 0.0 copy-done.6
  1.4 0.0 copy-done.7
  1.4 0.0 copy-start
  1.4 1.2 %copy-done = bf16[27,128,128]{2,1,0:T(8,128)(2,1)S(1)} copy-done((bf16[27,128,128]{2,1,0:T(8,128)(2,1)S(1)}, bf16[27,128,128]{2,1,0:T(8,128)(2,1)}, u32[]{:S(2)}) %copy-start) | copy-done | bytes 884760
  2.5 0.0 copy-start.1
  2.5 1.2 %copy-done.1 = bf16[27,128,128]{2,1,0:T(8,128)(2,1)S(1)} copy-done((bf16[27,128,128]{2,1,0:T(8,128)(2,1)S(1)}, bf16[27,128,128]{2,1,0:T(8,128)(2,1)}, u32[]{:S(2)}) %copy-start.1) | copy-done | bytes 884760
  3.7 0.0 copy-start.2
  3.7 0.9 %copy-done.2 = bf16[1,1,512,128]{3,2,1,0:T(8,128)(2,1)S(1)} copy-done((bf16[1,1,512,128]{3,2,1,0:T(8,128)(2,1)S(1)}, bf16[1,1,512,128]{3,2,1,0:T(8,128)(2,1)}, u32[]{:S(2)}) %copy-start.2) | copy-done | bytes 131096
  4.6 0.0 copy-start.3
  4.6 0.8 %copy-done.3 = s32[1,1,27,512]{3,1,2,0:T(1,128)S(1)} copy-done((s32[1,1,27,512]{3,1,2,0:T(1,128)S(1)}, s32[1,1,27,512]{3,1,2,0:T(1,128)}, u32[]{:S(2)}) %copy-start.3) | copy-done | bytes 55320
  5.4 23.6 %shard_map.100 = bf16[512,128]{1,0:T(8,128)(2,1)S(1)} custom-call(bf16[512,128]{1,0:T(8,128)(2,1)S(1)} %bitcast.13, s32[1,1]{1,0:T(1,128)S(6)} %copy.12.count_ref, s32[27,1,512]{2,1,0:T(1,128)S(1)} %bitcast.14, s32[4,64]{1,0:T(4,128)S(1)} %bitcast.15, f32[1,128]{1,0:T(1,128)S(1)} %bitcast.16, f32[1,128]{1,0:T(1,128)S(1)} %bitcast.17, f32[1,128]{1,0:T(1,128)S(1)} %bitcast.18, ...), custom_call_target="tpu_custom_call" | custom-call | tf_op jit(solution)/shard_map/pallas_call | solution.py:391
  29.1 0.7 %copy.13 = bf16[1,1,512,128]{3,2,1,0:T(8,128)(2,1)} copy(bf16[1,1,512,128]{3,2,1,0:T(8,128)(2,1)S(1)} %bitcast.12) | data formatting | bytes 262144
Async XLA Ops:
  0.7 0.7 %copy-start.8 = (f32[128]{0:T(128)S(1)}, f32[128]{0:T(128)}, u32[]{:S(2)}) copy-start(f32[128]{0:T(128)} %param.19) | copy-start | bytes 1540
  0.7 0.7 %copy-start.4 = (s32[1,1,4,64]{3,2,1,0:T(4,128)S(1)}, s32[1,1,4,64]{3,2,1,0:T(4,128)}, u32[]{:S(2)}) copy-start(s32[1,1,4,64]{3,2,1,0:T(4,128)} %param.13) | copy-start | bytes 3076
  0.7 0.7 %copy-start.5 = (f32[128]{0:T(128)S(1)}, f32[128]{0:T(128)}, u32[]{:S(2)}) copy-start(f32[128]{0:T(128)} %param.15) | copy-start | bytes 1540
  0.7 0.7 %copy-start.6 = (f32[128]{0:T(128)S(1)}, f32[128]{0:T(128)}, u32[]{:S(2)}) copy-start(f32[128]{0:T(128)} %param.16) | copy-start | bytes 1540
  0.7 0.7 %copy-start.7 = (f32[128]{0:T(128)S(1)}, f32[128]{0:T(128)}, u32[]{:S(2)}) copy-start(f32[128]{0:T(128)} %param.18) | copy-start | bytes 1540
  1.4 1.2 %copy-start = (bf16[27,128,128]{2,1,0:T(8,128)(2,1)S(1)}, bf16[27,128,128]{2,1,0:T(8,128)(2,1)}, u32[]{:S(2)}) copy-start(bf16[27,128,128]{2,1,0:T(8,128)(2,1)} %param.14) | copy-start | bytes 2654212
  2.5 1.2 %copy-start.1 = (bf16[27,128,128]{2,1,0:T(8,128)(2,1)S(1)}, bf16[27,128,128]{2,1,0:T(8,128)(2,1)}, u32[]{:S(2)}) copy-start(bf16[27,128,128]{2,1,0:T(8,128)(2,1)} %param.17) | copy-start | bytes 2654212
  3.7 0.9 %copy-start.2 = (bf16[1,1,512,128]{3,2,1,0:T(8,128)(2,1)S(1)}, bf16[1,1,512,128]{3,2,1,0:T(8,128)(2,1)}, u32[]{:S(2)}) copy-start(bf16[1,1,512,128]{3,2,1,0:T(8,128)(2,1)} %param.10) | copy-start | bytes 393220
  4.6 0.8 %copy-start.3 = (s32[1,1,27,512]{3,1,2,0:T(1,128)S(1)}, s32[1,1,27,512]{3,1,2,0:T(1,128)}, u32[]{:S(2)}) copy-start(s32[1,1,27,512]{3,1,2,0:T(1,128)} %param.12) | copy-start | bytes 165892

commit v2 on v1

--- a/solution.py
+++ b/solution.py
@@ -388,9 +388,10 @@
     vmem = pl.BlockSpec(memory_space=pltpu.VMEM)
     hbm = pl.BlockSpec(memory_space=pltpu.HBM)
     group = taps // 3 * channels
+    stay = partial(pltpu.with_memory_space_constraint, memory_space=pltpu.HBM)
     output = pl.pallas_call(
         partial(block_kernel, n_slab, n_tile),
-        out_shape=jax.ShapeDtypeStruct((rows, channels), features.dtype),
+        out_shape=pltpu.VMEM((rows, channels), features.dtype),
         in_specs=[hbm, smem] + [hbm] * 8,
         out_specs=vmem,
         scratch_shapes=[
@@ -425,19 +426,19 @@
             pltpu.SemaphoreType.DMA((3,)),
         ],
         compiler_params=pltpu.CompilerParams(
-            collective_id=0, has_side_effects=True, vmem_limit_bytes=30000000
+            collective_id=0, has_side_effects=True, vmem_limit_bytes=40000000
         ),
     )(
-        features[0, 0],
+        stay(features[0, 0]),
         counts,
-        rulebook.reshape(taps, 1, rows),
-        face_rows[0, 0],
-        gain_one[None],
-        shift_one[None],
-        gain_two[None],
-        shift_two[None],
-        conv_one.reshape(taps * channels, channels),
-        conv_two.reshape(taps * channels, channels),
+        stay(rulebook.reshape(taps, 1, rows)),
+        stay(face_rows[0, 0]),
+        stay(gain_one[None]),
+        stay(shift_one[None]),
+        stay(gain_two[None]),
+        stay(shift_two[None]),
+        stay(conv_one.reshape(taps * channels, channels)),
+        stay(conv_two.reshape(taps * channels, channels)),
     )
     return output[None, None]
 

time: 30 us -> 24.9 us (0.83)
  local copies, waits for them, and re-layouts: 5.39 us -> 0.66 us
    unnamed x19 -> x1, local copies, waits for them, and re-layouts: 5.39 us -> 0.66 us
where the time goes in v2:
time: 24.9 us; the launch traced here: 24.8 us
  Pallas kernels  23.4 us (94%)
  local copies, waits for them, and re-layouts  0.66 us (3%)
  between operations  0.66 us (3%)
    pallas_call x1, Pallas kernels, per_device(): pl.pallas_call(partial(block_kernel, n_slab, n_tile), out_shape=pltpu.VME...  23.4 us
    unnamed x1, local copies, waits for them, and re-layouts  0.66 us

profile of v2, /device:TPU:0, one launch (start us, length us, event | category | flops | bytes accessed | tf_op | source)
XLA Modules:
  0.0 24.8 jit_solution(5289908670531204456)
XLA Ops:
  0.7 23.4 %shard_map.100 = bf16[512,128]{1,0:T(8,128)(2,1)S(1)} custom-call(bf16[512,128]{1,0:T(8,128)(2,1)} %bitcast.13, s32[1,1]{1,0:T(1,128)S(6)} %copy.13.count_ref, s32[27,1,512]{2,1,0:T(1,128)} %bitcast.14, s32[4,64]{1,0:T(4,128)} %bitcast.15, f32[1,128]{1,0:T(1,128)} %bitcast.16, f32[1,128]{1,0:T(1,128)} %bitcast.17, f32[1,128]{1,0:T(1,128)} %bitcast.18, ...), custom_call_target="tpu_custom_call" | custom-call | tf_op jit(solution)/shard_map/pallas_call | solution.py:392
  24.1 0.7 %copy.12 = bf16[1,1,512,128]{3,2,1,0:T(8,128)(2,1)} copy(bf16[1,1,512,128]{3,2,1,0:T(8,128)(2,1)S(1)} %bitcast.10) | data formatting | bytes 262144

commit v3 on v2

v3 whole, which is shorter than its diff:
```python
from functools import partial

import jax
import jax.numpy as jnp
from jax import lax
from jax.experimental import pallas as pl
from jax.experimental.pallas import tpu as pltpu
from jax.sharding import PartitionSpec as P

EPSILON = 1e-05
MESH = pl.DeviceIdType.MESH
BLOCK = 256
PIECE = 16
LOWEST = -3e38
F32 = jnp.float32
BF16 = jnp.bfloat16


def transfers(face_len):
    low, high = 0, face_len
    edge = face_len - PIECE
    end = PIECE + face_len
    return (
        (1, 0, high, face_len, 0, 0),
        (-1, 0, low, face_len, 0, face_len),
        (0, 1, 3 * face_len, face_len, 1, PIECE),
        (0, -1, 2 * face_len, face_len, 2, PIECE),
        (1, 1, high + edge, PIECE, 1, 0),
        (-1, 1, low + edge, PIECE, 1, end),
        (1, -1, high, PIECE, 2, 0),
        (-1, -1, low, PIECE, 2, end),
    )


def tap_of(dx, dy, z):
    return 9 * (dx + 1) + 3 * (dy + 1) + z


def plane_size(n_slab):
    size = 1
    while 4 * size * size <= n_slab and n_slab % (2 * size) == 0:
        size *= 2
    return size


def block_kernel(
    n_slab,
    n_tile,
    feat_hbm,
    rule_hbm,
    face_hbm,
    gain_one_hbm,
    shift_one_hbm,
    gain_two_hbm,
    shift_two_hbm,
    conv_one_hbm,
    conv_two_hbm,
    out_ref,
    feat_ref,
    rule_ref,
    face_ref,
    gain_one_ref,
    shift_one_ref,
    gain_two_ref,
    shift_two_ref,
    weight_ref,
    weight_t_ref,
    side_weight_ref,
    onehot_ref,
    hot_ref,
    place_ref,
    part_ref,
    keep_ref,
    face_hot_ref,
    square_ref,
    corner_ref,
    edge_ref,
    side_ref,
    acc_ref,
    own_ref,
    send_ref,
    wide_send_ref,
    halo_ref,
    wide_halo_ref,
    lhs_ref,
    picked_ref,
    stats_one_ref,
    stats_two_ref,
    input_sem,
    send_sem,
    recv_sem,
    stat_send_sem,
    stat_recv_sem,
    ready_sem,
):
    rows, channels = feat_ref.shape
    taps = rule_ref.shape[0]
    face_len = face_ref.shape[1]
    side = rows // face_len
    column = face_len // side
    n_dev = n_slab * n_tile
    blocks = rows // BLOCK
    half = taps // 2
    wide = 2 * face_len
    slab = lax.axis_index("slab")
    tile = lax.axis_index("tile")
    me = slab * n_tile + tile

    def fetch(i, src, dst):
        return pltpu.make_async_copy(src, dst, input_sem.at[i])

    feat_copy = fetch(0, feat_hbm, feat_ref)
    face_copy = fetch(1, face_hbm, face_ref)
    rule_copy = fetch(2, rule_hbm, rule_ref)
    affine_copies = [
        fetch(3, gain_one_hbm, gain_one_ref),
        fetch(4, shift_one_hbm, shift_one_ref),
        fetch(5, gain_two_hbm, gain_two_ref),
        fetch(6, shift_two_hbm, shift_two_ref),
    ]
    weight_copies = [
        fetch(7, conv_one_hbm, weight_ref.at[0]),
        fetch(8, conv_two_hbm, weight_ref.at[1]),
    ]
    for copy in (face_copy, feat_copy, rule_copy):
        copy.start()
    halo_ref[...] = jnp.zeros_like(halo_ref)
    wide_halo_ref[...] = jnp.zeros_like(wide_halo_ref)

    def moved(place, step, size):
        if size & (size - 1) == 0:
            return place ^ step
        place = place + step
        return jnp.where(place >= size, place - size, place)

    def each_peer(act):
        for j in reversed(range(n_tile)):
            other = moved(tile, j, n_tile) if j else tile

            def visit(i, carry):
                act({"slab": moved(slab, n_slab - 1 - i, n_slab), "tile": other})
                return carry

            last = n_slab if j else n_slab - 1
            lax.fori_loop(0, last, visit, 0, unroll=n_slab <= 16)

    plane = plane_size(n_slab)
    within = slab % plane
    first_of_plane = slab - within

    def each_near(act):
        for i in range(n_slab // plane - 1, 0, -1):
            layer = moved(slab // plane, i, n_slab // plane)
            act({"slab": layer * plane + within, "tile": tile})
        for step, crosses in ((1, within == plane - 1), (-1, within == 0)):
            inside = (slab + step >= 0) & (slab + step < n_slab)
            for dt in (-1, 0, 1):
                there = inside & crosses & (tile + dt >= 0) & (tile + dt < n_tile)
                peer = {"slab": slab + step, "tile": tile + dt}
                pl.when(there)(partial(act, peer))
        for i in range(plane - 1, -1, -1):
            for j in range(n_tile - 1, -1, -1):
                if i or j:
                    other = first_of_plane + moved(within, i, plane)
                    act({"slab": other, "tile": moved(tile, j, n_tile) if j else tile})

    near_tiles = 1 + (tile > 0).astype(jnp.int32) + (tile < n_tile - 1).astype(jnp.int32)
    crossings = ((within == 0) & (slab > 0)).astype(jnp.int32) + (
        (within == plane - 1) & (slab < n_slab - 1)
    ).astype(jnp.int32)
    n_near = n_slab // plane - 1 + plane * n_tile - 1 + crossings * near_tiles

    barrier = pltpu.get_barrier_semaphore()
    each_near(
        lambda peer: pl.semaphore_signal(barrier, inc=1, device_id=peer, device_id_type=MESH)
    )
    for copy in weight_copies + affine_copies:
        copy.start()

    def halo(which, start):
        source, target = ((send_ref, halo_ref), (wide_send_ref, wide_halo_ref))[which]
        for j, (ds, dt, first, size, buffer, place) in enumerate(transfers(face_len)):
            copy = pltpu.make_async_remote_copy(
                src_ref=source.at[pl.ds(first, size)],
                dst_ref=target.at[buffer, pl.ds(place, size)],
                send_sem=send_sem.at[which, j],
                recv_sem=recv_sem.at[which, j],
                device_id={"slab": slab + ds, "tile": tile + dt},
                device_id_type=MESH,
            )
            sends, receives = True, True
            if ds > 0:
                sends, receives = slab < n_slab - 1, slab > 0
            elif ds < 0:
                sends, receives = slab > 0, slab < n_slab - 1
            if dt > 0:
                sends, receives = sends & (tile < n_tile - 1), receives & (tile > 0)
            elif dt < 0:
                sends, receives = sends & (tile > 0), receives & (tile < n_tile - 1)
            if start:
                pl.when(sends)(copy.start)
            else:
                pl.when(receives)(copy.wait_recv)
                pl.when(sends)(copy.wait_send)

    corner_ref[...] = jnp.zeros_like(corner_ref)
    edge_ref[...] = jnp.zeros_like(edge_ref)
    face_copy.wait()
    square_ref[...] = jnp.zeros_like(square_ref)
    square_ref[0:4, 0:face_len] = face_ref[...].astype(F32)
    face_cols = square_ref[...].T
    lane_rows = lax.broadcasted_iota(jnp.int32, (face_len, rows), 1)
    for k in range(4):
        wanted = face_cols[0:face_len, k : k + 1].astype(jnp.int32)
        face_hot_ref[k * face_len : (k + 1) * face_len, :] = jnp.where(
            lane_rows == wanted, 1.0, 0.0
        ).astype(BF16)

    feat_copy.wait()
    feat = feat_ref[...]
    send_ref[...] = jnp.dot(face_hot_ref[...], feat, preferred_element_type=F32).astype(BF16)

    pl.semaphore_wait(barrier, n_near)
    halo(0, True)
    each_near(
        lambda peer: pl.semaphore_signal(ready_sem, inc=1, device_id=peer, device_id_type=MESH)
    )

    for b in range(blocks):
        lhs_ref[b * channels : (b + 1) * channels, :] = feat[b * BLOCK : (b + 1) * BLOCK].T

    rule_copy.wait()
    rule = rule_ref[...]
    below = rows + 2 * face_len
    tile_len = face_len + 2 * column
    table = below + 2 * tile_len
    place_ref[...] = jnp.where(rule < rows, rule & (BLOCK - 1), -1).astype(F32)
    part_ref[...] = rule // BLOCK
    keep_ref[...] = jnp.where(rule < table, 1, 0)
    position = lax.broadcasted_iota(jnp.int32, (BLOCK, rows), 0).astype(F32).astype(BF16)
    one, none = jnp.ones((BLOCK, rows), BF16), jnp.zeros((BLOCK, rows), BF16)

    def hot(places, low, size):
        return jnp.where(
            position[low : low + size] == places.astype(F32).astype(BF16),
            one[0:size],
            none[0:size],
        )

    def side_hot(dx, dy, z, low):
        spot = rule_ref[tap_of(dx, dy, z)]
        places = jnp.full((1, rows), -1, jnp.int32)

        def fill(places, base, size, to):
            inside = (spot >= base) & (spot < base + size)
            return jnp.where(inside, spot - base + to, places)

        if dx:
            places = fill(places, rows + (face_len if dx > 0 else 0), face_len, low)
        if dy:
            start = below + (tile_len if dy > 0 else 0)
            places = fill(places, start + column, face_len, low + (face_len if dx else 0))
            if dx:
                end = column + face_len if dx > 0 else 0
                places = fill(
                    places, start + end, column, low + (face_len - column if dy < 0 else 0)
                )
        return hot(places, low, wide if dx and dy else face_len)

    live = keep_ref[half].astype(F32)
    count = jnp.sum(live, axis=1, keepdims=True)
    live_rows = (
        lax.broadcasted_iota(jnp.int32, (rows, 1), 0).astype(F32) < count
    ).astype(F32)

    def turn_weights(i):
        weight_copies[i].wait()
        for dx in (-1, 0, 1):
            for dy in (-1, 0, 1):
                for z in range(3):
                    tap = tap_of(dx, dy, z)
                    turned = weight_ref[i, tap * channels : (tap + 1) * channels, :].T
                    weight_t_ref[i, :, tap * channels : (tap + 1) * channels] = turned
                    if i == 0 and (dx or dy):
                        if dx and dy:
                            which, part = (dx + 1) // 2, (dy + 1) // 2
                        elif dx:
                            which, part = 2, (dx + 1) // 2
                        else:
                            which, part = 3, (dy + 1) // 2
                        side_weight_ref[
                            which,
                            z * channels : (z + 1) * channels,
                            part * channels : (part + 1) * channels,
                        ] = turned

    def choose(tap, found):
        value = found[0:channels]
        for b in range(1, blocks):
            value = jnp.where(part_ref[tap] == b, found[b * channels : (b + 1) * channels], value)
        return value

    def pick_local(build):
        def pick(h, carry):
            for j in range(half):
                tap = h * (half + 1) + j
                slot = h * half + j
                if build:
                    onehot_ref[slot] = jnp.where(position == place_ref[tap].astype(BF16), one, none)
                found = jnp.dot(lhs_ref[...], onehot_ref[slot], preferred_element_type=F32)
                picked_ref[tap] = choose(tap, found).astype(BF16)
            return carry

        lax.fori_loop(0, 2, pick, 0)

    pick_local(True)
    for b in range(blocks):
        picked_ref[half, :, b * BLOCK : (b + 1) * BLOCK] = lhs_ref[
            b * channels : (b + 1) * channels, :
        ]
    turn_weights(0)
    acc_ref[...] = jnp.dot(
        weight_t_ref[0], picked_ref[...].reshape(taps * channels, rows), preferred_element_type=F32
    )
    for z in range(3):
        for i, dx in enumerate((-1, 1)):
            for j, dy in enumerate((-1, 1)):
                hot_ref[3 * z + i, j * wide : (j + 1) * wide, :] = side_hot(dx, dy, z, j * wide)
        for j, (dx, dy) in enumerate(((-1, 0), (1, 0), (0, -1), (0, 1))):
            low = j * face_len
            hot_ref[3 * z + 2, low : low + face_len, :] = side_hot(dx, dy, z, low)

    sub = lax.broadcasted_iota(jnp.int32, (PIECE, channels), 0).astype(F32)
    ahead = (sub < column).astype(F32)

    def sides(pieces):
        slabs, low_tile, high_tile = pieces
        end = PIECE + face_len
        edge = face_len - PIECE

        def mix(upper, lower):
            dtype = upper.dtype
            upper, lower = upper.astype(F32), lower.astype(F32)
            return (upper * ahead + lower * (1.0 - ahead)).astype(dtype)

        corners, straight = [], []
        for i in range(2):
            own = slabs[i * face_len : (i + 1) * face_len]
            spot = slice(end, end + PIECE) if i else slice(0, PIECE)
            straight.append(own)
            corners.append(
                jnp.concatenate(
                    [own[0:edge], mix(own[edge:], low_tile[spot]), low_tile[PIECE:end]], axis=0
                )
            )
            corners.append(
                jnp.concatenate(
                    [mix(high_tile[spot], own[0:PIECE]), own[PIECE:], high_tile[PIECE:end]], axis=0
                )
            )
        straight.append(low_tile[PIECE:end])
        straight.append(high_tile[PIECE:end])
        return corners, straight

    across = (((1,), (1,)), ((), ()))

    def tell(which, buffer, values, more):
        kept = values * live_rows
        sums = [jnp.sum(kept, axis=0, keepdims=True), jnp.sum(kept * values, axis=0, keepdims=True)]
        buffer[me] = jnp.concatenate(sums + more, axis=0)
        mine = buffer.at[me]
        each_peer(
            lambda peer: pltpu.make_async_remote_copy(
                src_ref=mine,
                dst_ref=mine,
                send_sem=stat_send_sem.at[which],
                recv_sem=stat_recv_sem.at[which],
                device_id=peer,
                device_id_type=MESH,
            ).start()
        )
        return sums[0]

    def shared(which, buffer):
        others = buffer.at[pl.ds(0, n_dev - 1)]
        pltpu.make_async_copy(others, others, stat_recv_sem.at[which]).wait()
        pltpu.make_async_copy(others, others, stat_send_sem.at[which]).wait()
        return jnp.sum(buffer[...], axis=0)

    def spread(row):
        return jnp.broadcast_to(row, (channels, channels)).T

    def repeat(square):
        return jnp.concatenate([square] * (rows // channels), axis=1)

    halo(0, False)
    corners, straight = sides([halo_ref[i] for i in range(3)])
    for i in range(4):
        j = i % 2
        corner_ref[
            i // 2, j * wide : (j + 1) * wide, j * channels : (j + 1) * channels
        ] = corners[i]
        edge_ref[
            i // 2, j * face_len : (j + 1) * face_len, j * channels : (j + 1) * channels
        ] = straight[i]
    products = [
        lax.dot_general(
            side_weight_ref[i],
            corner_ref[i] if i < 2 else edge_ref[i - 2],
            across,
            preferred_element_type=F32,
        ).astype(BF16)
        for i in range(4)
    ]
    lhs = jnp.concatenate(
        [products[i][z * channels : (z + 1) * channels] for z in range(3) for i in range(4)], axis=1
    )
    first_t = acc_ref[...] + jnp.dot(
        lhs, hot_ref[...].reshape(9 * 2 * wide, rows), preferred_element_type=F32
    )
    acc_ref[...] = first_t
    first = first_t.T
    pl.semaphore_wait(ready_sem, n_near)
    counts = jnp.broadcast_to(count, (2, channels))
    centre = tell(0, stats_one_ref, first, [counts]) / count

    coarse = first.astype(BF16)
    fine = (first - coarse.astype(F32)).astype(BF16)
    both = jnp.dot(
        face_hot_ref[...],
        jnp.concatenate([coarse, fine], axis=1),
        preferred_element_type=F32,
    )
    wide_send_ref[...] = both[:, 0:channels] + both[:, channels:]
    halo(1, True)
    centred = acc_ref[...] - repeat(spread(centre))
    own_ref[...] = centred
    for b in range(blocks):
        lhs_ref[b * channels : (b + 1) * channels, :] = centred[
            :, b * BLOCK : (b + 1) * BLOCK
        ].astype(BF16)
    pick_local(False)
    turn_weights(1)
    for copy in affine_copies:
        copy.wait()

    def masked(tap, value):
        return jnp.where(keep_ref[tap] > 0, value, LOWEST).astype(BF16)

    for tap in (half - 1, half + 1):
        picked_ref[tap] = masked(tap, picked_ref[tap].astype(F32))
    halo(1, False)
    corners, straight = sides([(wide_halo_ref[i] - centre).astype(BF16) for i in range(3)])
    for i in range(4):
        side_ref[i] = corners[i].T
    lanes = lax.broadcasted_iota(jnp.int32, (channels, wide), 1)
    for i in range(2):
        turned = jnp.concatenate(straight[2 * i : 2 * i + 2], axis=0).astype(F32).T
        side_ref[4 + 2 * i] = jnp.where(lanes < face_len, turned, 0.0).astype(BF16)
        side_ref[5 + 2 * i] = jnp.where(lanes < face_len, 0.0, turned).astype(BF16)

    def add_side(tap, found):
        picked_ref[tap] = masked(tap, picked_ref[tap].astype(F32) + found)

    for z in range(3):
        for i, dx in enumerate((-1, 1)):
            for j, dy in enumerate((-1, 1)):
                spots = hot_ref[3 * z + i, j * wide : (j + 1) * wide, :]
                found = jnp.dot(side_ref[2 * i + j], spots, preferred_element_type=F32)
                add_side(tap_of(dx, dy, z), found)
        for i in range(2):
            spots = hot_ref[3 * z + 2, i * wide : (i + 1) * wide, :]
            pair = side_ref[4 + 2 * i : 6 + 2 * i].reshape(2 * channels, wide)
            found = jnp.dot(pair, spots, preferred_element_type=F32)
            for j, step in enumerate((-1, 1)):
                dx, dy = (0, step) if i else (step, 0)
                add_side(tap_of(dx, dy, z), found[j * channels : (j + 1) * channels])
    ratio = shift_one_ref[...] / gain_one_ref[...]

    total = shared(0, stats_one_ref)
    voxels = total[2:3]
    average = total[0:1] / voxels
    spread_one = total[1:2] / voxels - average * average + EPSILON
    inverse = lax.rsqrt(spread_one)
    scale = inverse * gain_one_ref[...]
    floor_col = spread(average - centre - ratio * (spread_one * inverse))
    scale_col = spread(scale)

    centre_value = jnp.maximum(own_ref[...], repeat(floor_col)) - repeat(floor_col)
    centre_value = jnp.where(keep_ref[half] > 0, centre_value * repeat(scale_col), 0.0)
    low = repeat(floor_col.astype(BF16))
    second_t = jnp.zeros((channels, rows), F32)
    group = taps // 3
    for x in range(3):
        taken, used = [], []
        for j in range(group):
            tap = x * group + j
            weight = weight_t_ref[1, :, tap * channels : (tap + 1) * channels]
            if tap == half:
                taken.append(centre_value.astype(BF16))
                used.append(weight)
            else:
                taken.append(jnp.maximum(picked_ref[tap], low) - low)
                used.append((weight.astype(F32) * scale).astype(BF16))
        second_t = second_t + jnp.dot(
            jnp.concatenate(used, axis=1),
            jnp.concatenate(taken, axis=0),
            preferred_element_type=F32,
        )
    second = second_t.T
    tell(1, stats_two_ref, second, [])
    total = shared(1, stats_two_ref)
    average = total[0:1] / voxels
    variance = total[1:2] / voxels - average * average
    scale = lax.rsqrt(variance + EPSILON) * gain_two_ref[...]
    offset = shift_two_ref[...] - average * scale
    summed = second * scale + offset + feat_ref[...].astype(F32)
    out_ref[...] = (live_rows * jnp.maximum(summed, 0.0)).astype(BF16)


def per_device(
    n_slab,
    n_tile,
    features,
    counts,
    rulebook,
    face_rows,
    conv_one,
    gain_one,
    shift_one,
    conv_two,
    gain_two,
    shift_two,
):
    rows, channels = features.shape[2:]
    taps = rulebook.shape[2]
    faces, face_len = face_rows.shape[2:]
    blocks = rows // BLOCK
    n_dev = n_slab * n_tile
    wide = 2 * face_len
    hbm = pl.BlockSpec(memory_space=pltpu.HBM)
    stay = partial(pltpu.with_memory_space_constraint, memory_space=pltpu.HBM)
    output = pl.pallas_call(
        partial(block_kernel, n_slab, n_tile),
        out_shape=pltpu.VMEM((rows, channels), features.dtype),
        in_specs=[hbm] * 9,
        out_specs=pl.BlockSpec(memory_space=pltpu.VMEM),
        scratch_shapes=[
            pltpu.VMEM((rows, channels), BF16),
            pltpu.VMEM((taps, 1, rows), jnp.int32),
            pltpu.VMEM((faces, face_len), jnp.int32),
            pltpu.VMEM((1, channels), F32),
            pltpu.VMEM((1, channels), F32),
            pltpu.VMEM((1, channels), F32),
            pltpu.VMEM((1, channels), F32),
            pltpu.VMEM((2, taps * channels, channels), BF16),
            pltpu.VMEM((2, channels, taps * channels), BF16),
            pltpu.VMEM((4, 3 * channels, 2 * channels), BF16),
            pltpu.VMEM((taps - 1, BLOCK, rows), BF16),
            pltpu.VMEM((9, 2 * wide, rows), BF16),
            pltpu.VMEM((taps, 1, rows), F32),
            pltpu.VMEM((taps, 1, rows), jnp.int32),
            pltpu.VMEM((taps, 1, rows), jnp.int32),
            pltpu.VMEM((faces * face_len, rows), BF16),
            pltpu.VMEM((channels, channels), F32),
            pltpu.VMEM((2, 2 * wide, 2 * channels), BF16),
            pltpu.VMEM((2, wide, 2 * channels), BF16),
            pltpu.VMEM((8, channels, wide), BF16),
            pltpu.VMEM((channels, rows), F32),
            pltpu.VMEM((channels, rows), F32),
            pltpu.VMEM((faces * face_len, channels), BF16),
            pltpu.VMEM((faces * face_len, channels), F32),
            pltpu.VMEM((3, BLOCK // 2, channels), BF16),
            pltpu.VMEM((3, BLOCK // 2, channels), F32),
            pltpu.VMEM((blocks * channels, BLOCK), BF16),
            pltpu.VMEM((taps, channels, rows), BF16),
            pltpu.VMEM((n_dev, 4, channels), F32),
            pltpu.VMEM((n_dev, 2, channels), F32),
            pltpu.SemaphoreType.DMA((9,)),
            pltpu.SemaphoreType.DMA((2, 8)),
            pltpu.SemaphoreType.DMA((2, 8)),
            pltpu.SemaphoreType.DMA((2,)),
            pltpu.SemaphoreType.DMA((2,)),
            pltpu.SemaphoreType.REGULAR,
        ],
        compiler_params=pltpu.CompilerParams(
            collective_id=0, has_side_effects=True, vmem_limit_bytes=48000000
        ),
    )(
        stay(features[0, 0]),
        stay(rulebook.reshape(taps, 1, rows)),
        stay(face_rows[0, 0]),
        stay(gain_one[None]),
        stay(shift_one[None]),
        stay(gain_two[None]),
        stay(shift_two[None]),
        stay(conv_one.reshape(taps * channels, channels)),
        stay(conv_two.reshape(taps * channels, channels)),
    )
    return output[None, None]


def solution(mesh):
    placed = (
        P("slab", "tile", None, None),
        P("slab", "tile"),
        P("slab", "tile", None, None),
        P("slab", "tile", None, None),
        P(),
        P(),
        P(),
        P(),
        P(),
        P(),
    )
    return jax.shard_map(
        partial(per_device, mesh.shape["slab"], mesh.shape["tile"]),
        mesh=mesh,
        in_specs=placed,
        out_specs=P("slab", "tile", None, None),
        check_vma=False,
    )
```

time: 24.9 us -> 21.4 us (0.86)
  Pallas kernels: 23.4 us -> 20.6 us
  between operations: 0.66 us -> 0.01 us
    pallas_call x1, Pallas kernels: 23.4 us -> 20.6 us  [per_device(): pl.pallas_call(partial(block_kernel, n_slab, n_tile), out_shape=pltpu.VME...]
where the time goes in v3:
time: 21.4 us; the launch traced here: 21.2 us
  Pallas kernels  20.6 us (96%)
  local copies, waits for them, and re-layouts  0.66 us (3%)
    pallas_call x1, Pallas kernels, per_device(): pl.pallas_call(partial(block_kernel, n_slab, n_tile), out_shape=pltpu.VME...  20.6 us
    unnamed x1, local copies, waits for them, and re-layouts  0.66 us

profile of v3, /device:TPU:0, one launch (start us, length us, event | category | flops | bytes accessed | tf_op | source)
XLA Modules:
  0.0 21.2 jit_solution(17220933218973255100)
XLA Ops:
  0.0 20.6 %shard_map.91 = bf16[512,128]{1,0:T(8,128)(2,1)S(1)} custom-call(bf16[512,128]{1,0:T(8,128)(2,1)} %bitcast.13, s32[27,1,512]{2,1,0:T(1,128)} %bitcast.14, s32[4,64]{1,0:T(4,128)} %bitcast.15, f32[1,128]{1,0:T(1,128)} %bitcast.16, f32[1,128]{1,0:T(1,128)} %bitcast.17, f32[1,128]{1,0:T(1,128)} %bitcast.18, f32[1,128]{1,0:T(1,128)} %bitcast.19, ...), custom_call_target="tpu_custom_call" | custom-call | tf_op jit(solution)/shard_map/pallas_call | solution.py:543
  20.6 0.7 %copy.11 = bf16[1,1,512,128]{3,2,1,0:T(8,128)(2,1)} copy(bf16[1,1,512,128]{3,2,1,0:T(8,128)(2,1)S(1)} %bitcast.10) | data formatting | bytes 262144

commit v4 on v3

--- a/solution.py
+++ b/solution.py
@@ -133,18 +133,19 @@
         place = place + step
         return jnp.where(place >= size, place - size, place)
 
-    def each_peer(act):
+    plane = plane_size(n_slab)
+
+    def each_peer(act, far):
         for j in reversed(range(n_tile)):
             other = moved(tile, j, n_tile) if j else tile
+            top, least = (n_slab - 1, plane) if far else (plane - 1, 0 if j else 1)
 
             def visit(i, carry):
-                act({"slab": moved(slab, n_slab - 1 - i, n_slab), "tile": other})
+                act({"slab": moved(slab, top - i, n_slab), "tile": other})
                 return carry
 
-            last = n_slab if j else n_slab - 1
-            lax.fori_loop(0, last, visit, 0, unroll=n_slab <= 16)
-
-    plane = plane_size(n_slab)
+            lax.fori_loop(0, top + 1 - least, visit, 0, unroll=n_slab <= 16)
+
     within = slab % plane
     first_of_plane = slab - within
 
@@ -177,9 +178,11 @@
     for copy in weight_copies + affine_copies:
         copy.start()
 
-    def halo(which, start):
+    def halo(which, act, chosen):
         source, target = ((send_ref, halo_ref), (wide_send_ref, wide_halo_ref))[which]
         for j, (ds, dt, first, size, buffer, place) in enumerate(transfers(face_len)):
+            if j not in chosen:
+                continue
             copy = pltpu.make_async_remote_copy(
                 src_ref=source.at[pl.ds(first, size)],
                 dst_ref=target.at[buffer, pl.ds(place, size)],
@@ -197,10 +200,11 @@
                 sends, receives = sends & (tile < n_tile - 1), receives & (tile > 0)
             elif dt < 0:
                 sends, receives = sends & (tile > 0), receives & (tile < n_tile - 1)
-            if start:
+            if act == "start":
                 pl.when(sends)(copy.start)
+            elif act == "receive":
+                pl.when(receives)(copy.wait_recv)
             else:
-                pl.when(receives)(copy.wait_recv)
                 pl.when(sends)(copy.wait_send)
 
     corner_ref[...] = jnp.zeros_like(corner_ref)
@@ -220,15 +224,6 @@
     feat = feat_ref[...]
     send_ref[...] = jnp.dot(face_hot_ref[...], feat, preferred_element_type=F32).astype(BF16)
 
-    pl.semaphore_wait(barrier, n_near)
-    halo(0, True)
-    each_near(
-        lambda peer: pl.semaphore_signal(ready_sem, inc=1, device_id=peer, device_id_type=MESH)
-    )
-
-    for b in range(blocks):
-        lhs_ref[b * channels : (b + 1) * channels, :] = feat[b * BLOCK : (b + 1) * BLOCK].T
-
     rule_copy.wait()
     rule = rule_ref[...]
     below = rows + 2 * face_len
@@ -273,26 +268,31 @@
         lax.broadcasted_iota(jnp.int32, (rows, 1), 0).astype(F32) < count
     ).astype(F32)
 
-    def turn_weights(i):
-        weight_copies[i].wait()
-        for dx in (-1, 0, 1):
-            for dy in (-1, 0, 1):
-                for z in range(3):
-                    tap = tap_of(dx, dy, z)
-                    turned = weight_ref[i, tap * channels : (tap + 1) * channels, :].T
-                    weight_t_ref[i, :, tap * channels : (tap + 1) * channels] = turned
-                    if i == 0 and (dx or dy):
-                        if dx and dy:
-                            which, part = (dx + 1) // 2, (dy + 1) // 2
-                        elif dx:
-                            which, part = 2, (dx + 1) // 2
-                        else:
-                            which, part = 3, (dy + 1) // 2
-                        side_weight_ref[
-                            which,
-                            z * channels : (z + 1) * channels,
-                            part * channels : (part + 1) * channels,
-                        ] = turned
+    pl.semaphore_wait(barrier, n_near)
+    halo(0, "start", range(8))
+    each_near(
+        lambda peer: pl.semaphore_signal(ready_sem, inc=1, device_id=peer, device_id_type=MESH)
+    )
+
+    for b in range(blocks):
+        lhs_ref[b * channels : (b + 1) * channels, :] = feat[b * BLOCK : (b + 1) * BLOCK].T
+
+    def turn_weight(i, tap):
+        dx, dy, z = tap // 9 - 1, tap // 3 % 3 - 1, tap % 3
+        turned = weight_ref[i, tap * channels : (tap + 1) * channels, :].T
+        weight_t_ref[i, :, tap * channels : (tap + 1) * channels] = turned
+        if i == 0 and (dx or dy):
+            if dx and dy:
+                which, part = (dx + 1) // 2, (dy + 1) // 2
+            elif dx:
+                which, part = 2, (dx + 1) // 2
+            else:
+                which, part = 3, (dy + 1) // 2
+            side_weight_ref[
+                which,
+                z * channels : (z + 1) * channels,
+                part * channels : (part + 1) * channels,
+            ] = turned
 
     def choose(tap, found):
         value = found[0:channels]
@@ -300,35 +300,36 @@
             value = jnp.where(part_ref[tap] == b, found[b * channels : (b + 1) * channels], value)
         return value
 
-    def pick_local(build):
-        def pick(h, carry):
-            for j in range(half):
-                tap = h * (half + 1) + j
-                slot = h * half + j
-                if build:
-                    onehot_ref[slot] = jnp.where(position == place_ref[tap].astype(BF16), one, none)
-                found = jnp.dot(lhs_ref[...], onehot_ref[slot], preferred_element_type=F32)
-                picked_ref[tap] = choose(tap, found).astype(BF16)
-            return carry
-
-        lax.fori_loop(0, 2, pick, 0)
-
-    pick_local(True)
+    def build_side(tap):
+        dx, dy, z = tap // 9 - 1, tap // 3 % 3 - 1, tap % 3
+        i, j = (dx + 1) // 2, (dy + 1) // 2
+        if dx and dy:
+            hot_ref[3 * z + i, j * wide : (j + 1) * wide, :] = side_hot(dx, dy, z, j * wide)
+        elif dx or dy:
+            low = (i if dx else 2 + j) * face_len
+            hot_ref[3 * z + 2, low : low + face_len, :] = side_hot(dx, dy, z, low)
+
+    def pick_local(which):
+        for tap in range(taps):
+            turn_weight(which, tap)
+            if tap == half:
+                continue
+            slot = tap - (tap > half)
+            if which == 0:
+                onehot_ref[slot] = jnp.where(position == place_ref[tap].astype(BF16), one, none)
+                build_side(tap)
+            found = jnp.dot(lhs_ref[...], onehot_ref[slot], preferred_element_type=F32)
+            picked_ref[tap] = choose(tap, found).astype(BF16)
+
+    weight_copies[0].wait()
+    pick_local(0)
     for b in range(blocks):
         picked_ref[half, :, b * BLOCK : (b + 1) * BLOCK] = lhs_ref[
             b * channels : (b + 1) * channels, :
         ]
-    turn_weights(0)
     acc_ref[...] = jnp.dot(
         weight_t_ref[0], picked_ref[...].reshape(taps * channels, rows), preferred_element_type=F32
     )
-    for z in range(3):
-        for i, dx in enumerate((-1, 1)):
-            for j, dy in enumerate((-1, 1)):
-                hot_ref[3 * z + i, j * wide : (j + 1) * wide, :] = side_hot(dx, dy, z, j * wide)
-        for j, (dx, dy) in enumerate(((-1, 0), (1, 0), (0, -1), (0, 1))):
-            low = j * face_len
-            hot_ref[3 * z + 2, low : low + face_len, :] = side_hot(dx, dy, z, low)
 
     sub = lax.broadcasted_iota(jnp.int32, (PIECE, channels), 0).astype(F32)
     ahead = (sub < column).astype(F32)
@@ -364,10 +365,13 @@
 
     across = (((1,), (1,)), ((), ()))
 
-    def tell(which, buffer, values, more):
+    def tell(buffer, values, more):
         kept = values * live_rows
         sums = [jnp.sum(kept, axis=0, keepdims=True), jnp.sum(kept * values, axis=0, keepdims=True)]
         buffer[me] = jnp.concatenate(sums + more, axis=0)
+        return sums[0]
+
+    def share(which, buffer, far):
         mine = buffer.at[me]
         each_peer(
             lambda peer: pltpu.make_async_remote_copy(
@@ -377,9 +381,9 @@
                 recv_sem=stat_recv_sem.at[which],
                 device_id=peer,
                 device_id_type=MESH,
-            ).start()
+            ).start(),
+            far,
         )
-        return sums[0]
 
     def shared(which, buffer):
         others = buffer.at[pl.ds(0, n_dev - 1)]
@@ -393,7 +397,8 @@
     def repeat(square):
         return jnp.concatenate([square] * (rows // channels), axis=1)
 
-    halo(0, False)
+    halo(0, "receive", range(8))
+    halo(0, "sent", range(8))
     corners, straight = sides([halo_ref[i] for i in range(3)])
     for i in range(4):
         j = i % 2
@@ -422,7 +427,7 @@
     first = first_t.T
     pl.semaphore_wait(ready_sem, n_near)
     counts = jnp.broadcast_to(count, (2, channels))
-    centre = tell(0, stats_one_ref, first, [counts]) / count
+    centre = tell(stats_one_ref, first, [counts]) / count
 
     coarse = first.astype(BF16)
     fine = (first - coarse.astype(F32)).astype(BF16)
@@ -431,16 +436,18 @@
         jnp.concatenate([coarse, fine], axis=1),
         preferred_element_type=F32,
     )
+    share(0, stats_one_ref, True)
     wide_send_ref[...] = both[:, 0:channels] + both[:, channels:]
-    halo(1, True)
+    halo(1, "start", range(8))
+    share(0, stats_one_ref, False)
     centred = acc_ref[...] - repeat(spread(centre))
     own_ref[...] = centred
     for b in range(blocks):
         lhs_ref[b * channels : (b + 1) * channels, :] = centred[
             :, b * BLOCK : (b + 1) * BLOCK
         ].astype(BF16)
-    pick_local(False)
-    turn_weights(1)
+    weight_copies[1].wait()
+    pick_local(1)
     for copy in affine_copies:
         copy.wait()
 
@@ -449,32 +456,43 @@
 
     for tap in (half - 1, half + 1):
         picked_ref[tap] = masked(tap, picked_ref[tap].astype(F32))
-    halo(1, False)
-    corners, straight = sides([(wide_halo_ref[i] - centre).astype(BF16) for i in range(3)])
+    lanes = lax.broadcasted_iota(jnp.int32, (channels, wide), 1)
+
+    def add_side(tap, found):
+        picked_ref[tap] = masked(tap, picked_ref[tap].astype(F32) + found)
+
+    def pick_straight(i, own):
+        turned = jnp.concatenate(own, axis=0).astype(F32).T
+        side_ref[4 + 2 * i] = jnp.where(lanes < face_len, turned, 0.0).astype(BF16)
+        side_ref[5 + 2 * i] = jnp.where(lanes < face_len, 0.0, turned).astype(BF16)
+        for z in range(3):
+            spots = hot_ref[3 * z + 2, i * wide : (i + 1) * wide, :]
+            pair = side_ref[4 + 2 * i : 6 + 2 * i].reshape(2 * channels, wide)
+            found = jnp.dot(pair, spots, preferred_element_type=F32)
+            for j, step in enumerate((-1, 1)):
+                dx, dy = (0, step) if i else (step, 0)
+                add_side(tap_of(dx, dy, z), found[j * channels : (j + 1) * channels])
+
+    def received(i):
+        return (wide_halo_ref[i] - centre).astype(BF16)
+
+    halo(1, "receive", (2, 3))
+    pick_straight(
+        1, [(wide_halo_ref[i, PIECE : PIECE + face_len] - centre).astype(BF16) for i in (1, 2)]
+    )
+    halo(1, "receive", (0, 1))
+    pick_straight(0, [received(0)])
+    halo(1, "receive", (4, 5, 6, 7))
+    corners, _ = sides([received(i) for i in range(3)])
     for i in range(4):
         side_ref[i] = corners[i].T
-    lanes = lax.broadcasted_iota(jnp.int32, (channels, wide), 1)
-    for i in range(2):
-        turned = jnp.concatenate(straight[2 * i : 2 * i + 2], axis=0).astype(F32).T
-        side_ref[4 + 2 * i] = jnp.where(lanes < face_len, turned, 0.0).astype(BF16)
-        side_ref[5 + 2 * i] = jnp.where(lanes < face_len, 0.0, turned).astype(BF16)
-
-    def add_side(tap, found):
-        picked_ref[tap] = masked(tap, picked_ref[tap].astype(F32) + found)
-
     for z in range(3):
         for i, dx in enumerate((-1, 1)):
             for j, dy in enumerate((-1, 1)):
                 spots = hot_ref[3 * z + i, j * wide : (j + 1) * wide, :]
                 found = jnp.dot(side_ref[2 * i + j], spots, preferred_element_type=F32)
                 add_side(tap_of(dx, dy, z), found)
-        for i in range(2):
-            spots = hot_ref[3 * z + 2, i * wide : (i + 1) * wide, :]
-            pair = side_ref[4 + 2 * i : 6 + 2 * i].reshape(2 * channels, wide)
-            found = jnp.dot(pair, spots, preferred_element_type=F32)
-            for j, step in enumerate((-1, 1)):
-                dx, dy = (0, step) if i else (step, 0)
-                add_side(tap_of(dx, dy, z), found[j * channels : (j + 1) * channels])
+    halo(1, "sent", range(8))
     ratio = shift_one_ref[...] / gain_one_ref[...]
 
     total = shared(0, stats_one_ref)
@@ -489,26 +507,22 @@
     centre_value = jnp.maximum(own_ref[...], repeat(floor_col)) - repeat(floor_col)
     centre_value = jnp.where(keep_ref[half] > 0, centre_value * repeat(scale_col), 0.0)
     low = repeat(floor_col.astype(BF16))
-    second_t = jnp.zeros((channels, rows), F32)
-    group = taps // 3
-    for x in range(3):
-        taken, used = [], []
-        for j in range(group):
-            tap = x * group + j
-            weight = weight_t_ref[1, :, tap * channels : (tap + 1) * channels]
-            if tap == half:
-                taken.append(centre_value.astype(BF16))
-                used.append(weight)
-            else:
-                taken.append(jnp.maximum(picked_ref[tap], low) - low)
-                used.append((weight.astype(F32) * scale).astype(BF16))
-        second_t = second_t + jnp.dot(
-            jnp.concatenate(used, axis=1),
-            jnp.concatenate(taken, axis=0),
-            preferred_element_type=F32,
-        )
+    taken, used = [], []
+    for tap in range(taps):
+        weight = weight_t_ref[1, :, tap * channels : (tap + 1) * channels]
+        if tap == half:
+            taken.append(centre_value.astype(BF16))
+            used.append(weight)
+        else:
+            taken.append(jnp.maximum(picked_ref[tap], low) - low)
+            used.append((weight.astype(F32) * scale).astype(BF16))
+    second_t = jnp.dot(
+        jnp.concatenate(used, axis=1), jnp.concatenate(taken, axis=0), preferred_element_type=F32
+    )
     second = second_t.T
-    tell(1, stats_two_ref, second, [])
+    tell(stats_two_ref, second, [])
+    share(1, stats_two_ref, True)
+    share(1, stats_two_ref, False)
     total = shared(1, stats_two_ref)
     average = total[0:1] / voxels
     variance = total[1:2] / voxels - average * average

time: 21.4 us -> 20.8 us (0.972)
  Pallas kernels: 20.6 us -> 20 us
    pallas_call x1, Pallas kernels: 20.6 us -> 20 us  [per_device(): pl.pallas_call(partial(block_kernel, n_slab, n_tile), out_shape=pltpu.VME...]
where the time goes in v4:
time: 20.8 us; the launch traced here: 20.6 us
  Pallas kernels  20 us (96%)
  local copies, waits for them, and re-layouts  0.66 us (3%)
    pallas_call x1, Pallas kernels, per_device(): pl.pallas_call(partial(block_kernel, n_slab, n_tile), out_shape=pltpu.VME...  20 us
    unnamed x1, local copies, waits for them, and re-layouts  0.66 us

profile of v4, /device:TPU:0, one launch (start us, length us, event | category | flops | bytes accessed | tf_op | source)
XLA Modules:
  0.0 20.6 jit_solution(7563439080888620914)
XLA Ops:
  0.0 20.0 %shard_map.91 = bf16[512,128]{1,0:T(8,128)(2,1)S(1)} custom-call(bf16[512,128]{1,0:T(8,128)(2,1)} %bitcast.13, s32[27,1,512]{2,1,0:T(1,128)} %bitcast.14, s32[4,64]{1,0:T(4,128)} %bitcast.15, f32[1,128]{1,0:T(1,128)} %bitcast.16, f32[1,128]{1,0:T(1,128)} %bitcast.17, f32[1,128]{1,0:T(1,128)} %bitcast.18, f32[1,128]{1,0:T(1,128)} %bitcast.19, ...), custom_call_target="tpu_custom_call" | custom-call | tf_op jit(solution)/shard_map/pallas_call | solution.py:557
  20.0 0.7 %copy.11 = bf16[1,1,512,128]{3,2,1,0:T(8,128)(2,1)} copy(bf16[1,1,512,128]{3,2,1,0:T(8,128)(2,1)S(1)} %bitcast.10) | data formatting | bytes 262144

commit v5 on v4

--- a/solution.py
+++ b/solution.py
@@ -224,6 +224,12 @@
     feat = feat_ref[...]
     send_ref[...] = jnp.dot(face_hot_ref[...], feat, preferred_element_type=F32).astype(BF16)
 
+    pl.semaphore_wait(barrier, n_near)
+    halo(0, "start", range(8))
+    each_near(
+        lambda peer: pl.semaphore_signal(ready_sem, inc=1, device_id=peer, device_id_type=MESH)
+    )
+
     rule_copy.wait()
     rule = rule_ref[...]
     below = rows + 2 * face_len
@@ -267,12 +273,6 @@
     live_rows = (
         lax.broadcasted_iota(jnp.int32, (rows, 1), 0).astype(F32) < count
     ).astype(F32)
-
-    pl.semaphore_wait(barrier, n_near)
-    halo(0, "start", range(8))
-    each_near(
-        lambda peer: pl.semaphore_signal(ready_sem, inc=1, device_id=peer, device_id_type=MESH)
-    )
 
     for b in range(blocks):
         lhs_ref[b * channels : (b + 1) * channels, :] = feat[b * BLOCK : (b + 1) * BLOCK].T
@@ -370,6 +370,12 @@
         sums = [jnp.sum(kept, axis=0, keepdims=True), jnp.sum(kept * values, axis=0, keepdims=True)]
         buffer[me] = jnp.concatenate(sums + more, axis=0)
         return sums[0]
+
+    def fold(values):
+        parts = [values[:, i : i + channels] for i in range(0, rows, channels)]
+        while len(parts) > 1:
+            parts = [sum(parts[i : i + 2]) for i in range(0, len(parts), 2)]
+        return parts[0]
 
     def share(which, buffer, far):
         mine = buffer.at[me]
@@ -519,10 +525,14 @@
     second_t = jnp.dot(
         jnp.concatenate(used, axis=1), jnp.concatenate(taken, axis=0), preferred_element_type=F32
     )
-    second = second_t.T
-    tell(stats_two_ref, second, [])
+    kept = second_t * live
+    sums = jnp.sum(
+        jnp.concatenate([fold(kept), fold(kept * second_t)], axis=0).T, axis=0, keepdims=True
+    )
+    stats_two_ref[me] = jnp.concatenate([sums[:, 0:channels], sums[:, channels:]], axis=0)
     share(1, stats_two_ref, True)
     share(1, stats_two_ref, False)
+    second = second_t.T
     total = shared(1, stats_two_ref)
     average = total[0:1] / voxels
     variance = total[1:2] / voxels - average * average

time: 20.8 us -> 20.6 us (level)
  no operation moved by 1% of the time
where the time goes in v5:
time: 20.6 us; the launch traced here: 20.5 us
  Pallas kernels  19.8 us (96%)
  local copies, waits for them, and re-layouts  0.66 us (3%)
    pallas_call x1, Pallas kernels, per_device(): pl.pallas_call(partial(block_kernel, n_slab, n_tile), out_shape=pltpu.VME...  19.8 us
    unnamed x1, local copies, waits for them, and re-layouts  0.66 us

profile of v5, /device:TPU:0, one launch (start us, length us, event | category | flops | bytes accessed | tf_op | source)
XLA Modules:
  0.0 20.5 jit_solution(2303756921460043939)
XLA Ops:
  0.0 19.8 %shard_map.91 = bf16[512,128]{1,0:T(8,128)(2,1)S(1)} custom-call(bf16[512,128]{1,0:T(8,128)(2,1)} %bitcast.13, s32[27,1,512]{2,1,0:T(1,128)} %bitcast.14, s32[4,64]{1,0:T(4,128)} %bitcast.15, f32[1,128]{1,0:T(1,128)} %bitcast.16, f32[1,128]{1,0:T(1,128)} %bitcast.17, f32[1,128]{1,0:T(1,128)} %bitcast.18, f32[1,128]{1,0:T(1,128)} %bitcast.19, ...), custom_call_target="tpu_custom_call" | custom-call | tf_op jit(solution)/shard_map/pallas_call | solution.py:567
  19.8 0.7 %copy.11 = bf16[1,1,512,128]{3,2,1,0:T(8,128)(2,1)} copy(bf16[1,1,512,128]{3,2,1,0:T(8,128)(2,1)S(1)} %bitcast.10) | data formatting | bytes 262144
